TPU v7x, 32 devices: a whole 2x2x4 slice. The times are simulated.
32 devices in a mesh: pw: 8 (over z, core), band: 4 (over y, x).
Axes of the slice: x: 2, y: 2, z: 4, core: 2. Of those that a mesh axis runs over, the one named last changes fastest.
Arguments:
- wavefunctions: bfloat16 [2, 4096, 512], P(None, 'pw', 'band'), may hold values from -0.09375 to 0.09375
- miller: int32 [3, 4096], P(None, 'pw'), may hold values from -16 to 16
- reciprocal: float32 [3, 3], replicated, may hold values from -0.15 to 1.15, as said below
- fractional: float32 [3, 32], replicated, may hold values from 0 to 1
- species: int32 [32], replicated, may hold values from 0 to 3
- atom_order: int32 [32], replicated, may hold values from 0 to 31, each once
- radial_widths: float32 [4, 4], replicated, may hold values from 0.003 to 0.02
- onsite_base: float32 [4, 8, 8], replicated, may hold values from -2 to 2
- coupling: float32 [4, 64, 64], replicated, may hold values from -0.75 to 0.75
- occupations: float32 [512], P('band'), may hold values from 0 to 3, as said below
Outputs:
- applied: bfloat16 [2, 4096, 512], P(None, 'pw', 'band')
- onsite_d: float32 [32, 8, 8], P('pw')
Inputs may be any that keep to these rules, and one draw needn't show every extreme that they name: `atom_order`: a permutation of the atoms. `reciprocal`: each diagonal entry is 0.85 or more and each other entry 0.15 or less in magnitude. `occupations`: positive.
All inputs are finite; a program needn't handle non-finite values.
Results may differ from a plain program's by a relative error of at most 0.008.
Values may be sent and summed in bfloat16 or wider, within the bound.
A program may use at most 64 MiB of HBM per device.

v0:
```python
import functools
import math

import jax
import jax.numpy as jnp
import numpy as np
from jax import lax
from jax.experimental import pallas as pl
from jax.experimental.pallas import tpu as pltpu
from jax.sharding import PartitionSpec as P

MESH = pl.DeviceIdType.MESH
HIGH = lax.Precision.HIGHEST
BF = jnp.bfloat16
F32 = jnp.float32


def even_fit(function, degree):
    nodes = 0.125 + 0.125 * np.cos(np.pi * (np.arange(64) + 0.5) / 64)
    fit = np.polynomial.Chebyshev.fit(nodes, function(np.sqrt(nodes)), degree, domain=[0.0, 0.25])
    return [float(c) for c in fit.convert(kind=np.polynomial.Polynomial, domain=[-1, 1]).coef]


COS = even_fit(lambda t: np.cos(2 * np.pi * t), 7)
SIN = even_fit(lambda t: np.sin(2 * np.pi * t) / t, 7)


def series(coefs, u):
    value = jnp.full_like(u, coefs[-1])
    for c in coefs[-2::-1]:
        value = value * u + c
    return value


def iota(shape, dim):
    return lax.broadcasted_iota(jnp.int32, shape, dim)


def kernel(
    n,
    nb,
    wave,
    miller_h,
    reciprocal_h,
    fractional_h,
    species_h,
    order_h,
    widths_h,
    base_h,
    coupling_h,
    occ_h,
    applied,
    onsite,
    miller,
    reciprocal,
    fractional,
    species,
    order,
    widths,
    base,
    coupling,
    occ,
    wv,
    xs,
    cs,
    sn,
    amp,
    beta,
    beta_t,
    part,
    rs_in,
    p_all,
    o_in,
    o_sum,
    respond,
    ww,
    load_sem,
    rs_s,
    rs_r,
    ag_s,
    ag_r,
    oc_s,
    oc_r,
    ready,
):
    me = lax.axis_index("pw")
    mb = lax.axis_index("band")
    npw = wave.shape[1]
    bands = wave.shape[2]
    atoms = order.shape[0]
    kinds = widths.shape[0]
    own = atoms // n
    pack = own // 2
    rows = own * 8
    every = atoms * 8
    peers = n * nb

    small = [
        (miller_h, miller),
        (reciprocal_h, reciprocal),
        (fractional_h, fractional),
        (species_h, species),
        (order_h, order),
        (widths_h, widths),
        (base_h, base),
        (coupling_h, coupling),
        (occ_h, occ),
        (wave.at[0], wv.at[pl.ds(0, npw), pl.ds(0, bands)]),
        (wave.at[1], wv.at[pl.ds(0, npw), pl.ds(bands, bands)]),
        (wave.at[1], wv.at[pl.ds(npw, npw), pl.ds(0, bands)]),
    ]
    loads = [
        pltpu.make_async_copy(source, to, load_sem.at[i]) for i, (source, to) in enumerate(small)
    ]
    for copy in loads:
        copy.start()
    barrier = pltpu.get_barrier_semaphore()

    def place(q):
        return {"pw": lax.rem(me + q // nb, n), "band": lax.rem(mb + lax.rem(q, nb), nb)}

    def each(step):
        if peers <= 64:
            for q in range(1, peers):
                step(q)
        else:
            lax.fori_loop(1, peers, lambda q, carry: (step(q), carry)[1], 0)

    for d in range(1, n):
        pl.semaphore_signal(
            barrier, inc=1, device_id={"pw": lax.rem(me + d, n)}, device_id_type=MESH
        )
    for b in range(1, nb):
        pl.semaphore_signal(
            barrier, inc=1, device_id={"band": lax.rem(mb + b, nb)}, device_id_type=MESH
        )
    for copy in loads[0:6]:
        copy.wait()

    m = [miller[c : c + 1, :].astype(F32) for c in range(3)]
    g = [
        (2.0 * math.pi)
        * (reciprocal[c, 0] * m[0] + reciprocal[c, 1] * m[1] + reciprocal[c, 2] * m[2])
        for c in range(3)
    ]
    g2 = g[0] * g[0] + g[1] * g[1] + g[2] * g[2]
    j = iota((8, npw), 0)
    is_s = j < 2
    wide = [jnp.broadcast_to(v, (8, npw)) for v in g]
    factor = jnp.where(
        (j == 2) | (j == 5), wide[0], jnp.where((j == 3) | (j == 6), wide[1], wide[2])
    )
    half = jnp.broadcast_to(-0.5 * g2, (8, npw))
    for s in range(widths.shape[0]):
        w = jnp.where(
            j == 0,
            widths[s, 0],
            jnp.where(j == 1, widths[s, 1], jnp.where(j < 5, widths[s, 2], widths[s, 3])),
        )
        amp[s] = jnp.where(is_s, 1.0, factor * w) * jnp.exp(half * (w * w))

    def position(k, carry):
        a = order[k]
        xs[pl.ds(k, 1), :] = (
            fractional[0, a] * m[0] + fractional[1, a] * m[1] + fractional[2, a] * m[2]
        )
        return carry

    lax.fori_loop(0, atoms, position, 0, unroll=8)
    x = xs[...]
    t = x - jnp.round(x)
    u = t * t
    cs[...] = series(COS, u)
    sn[...] = t * series(SIN, u)

    def projector(pair, carry):
        real, imag = [], []
        for e in range(2):
            k = pair * 2 + e
            c = jnp.broadcast_to(cs[pl.ds(k, 1), :], (8, npw))
            s = jnp.broadcast_to(sn[pl.ds(k, 1), :], (8, npw))
            a = amp[species[order[k]]]
            real.append(a * jnp.where(is_s, c, -s))
            imag.append(-a * jnp.where(is_s, s, c))
        at = pl.ds(pl.multiple_of(pair * 16, 16), 16)
        beta[at, 0:npw] = jnp.concatenate(real, axis=0).astype(BF)
        beta[at, npw : 2 * npw] = jnp.concatenate(imag, axis=0).astype(BF)
        return carry

    lax.fori_loop(0, atoms // 2, projector, 0, unroll=4)

    for copy in loads[6:]:
        copy.wait()
    wv[npw : 2 * npw, bands : 2 * bands] = -wv[0:npw, 0:bands]
    part[...] = jnp.dot(beta[...], wv[...], preferred_element_type=F32).astype(BF)
    pl.semaphore_wait(barrier, n - 1 + nb - 1)

    def block(index):
        return pl.ds(pl.multiple_of(index * rows, rows), rows)

    def scatter(s):
        to = lax.rem(me + s, n)
        return pltpu.make_async_remote_copy(
            src_ref=part.at[block(to)],
            dst_ref=rs_in.at[s],
            send_sem=rs_s.at[s],
            recv_sem=rs_r.at[s],
            device_id={"pw": to},
            device_id_type=MESH,
        )

    upper_half = me // (n // 2)
    far_first = [
        lax.rem(n - 2 - me + upper_half + (2 * upper_half - 1) * i + 2 * (n - 1), n - 1) + 1
        for i in range(n - 1)
    ]
    sends = [scatter(s) for s in range(1, n)]
    for s in far_first:
        scatter(s).start()
    for b in range(1, nb):
        pl.semaphore_signal(
            ready, inc=1, device_id={"band": lax.rem(mb + b, nb)}, device_id_type=MESH
        )

    beta_t[:, 0:every] = beta[:, 0:npw].T
    beta_t[:, every : 2 * every] = beta[:, npw : 2 * npw].T
    weights = occ[...] * (1.0 / (bands * nb))
    weights = jnp.concatenate([weights, weights], axis=1)
    spread = (
        (iota((rows, own * 64), 0) // 8 == iota((rows, own * 64), 1) // 64)
        & (iota((rows, own * 64), 0) % 8 == iota((rows, own * 64), 1) % 8)
    ).astype(F32)
    row_of = (iota((8, own * 64), 1) % 64) // 8 == iota((8, own * 64), 0)
    diagonal = iota((rows, rows), 0) // 8 == iota((rows, rows), 1) // 8
    gather = (iota((128, rows), 0) % 8 == iota((128, rows), 1) % 8).astype(BF)
    flipped = coupling[...].reshape(kinds * 64, 64).T
    upper = flipped.astype(BF)
    lower = (flipped - upper.astype(F32)).astype(BF)
    none = jnp.zeros_like(upper)
    for i, piece in enumerate((upper, upper, lower)):
        respond[i * 128 : i * 128 + 64, :] = jnp.concatenate([piece, none], axis=1)
        respond[i * 128 + 64 : i * 128 + 128, :] = jnp.concatenate([none, piece], axis=1)
    line = iota((n * pack, 64), 0)
    kind_of = []
    for parity in range(2):
        column = jnp.zeros((n * pack, 64), jnp.int32)
        for row in range(n * pack):
            owner = lax.rem(me - row // pack + n, n)
            kind = species[order[owner * own + (row % pack) * 2 + parity]]
            column = jnp.where(line == row, kind, column)
        kind_of.append(column)
    fan = (iota((8, 64), 1) % 8 == iota((8, 64), 0)).astype(F32)
    mine = iota((8, 64), 1) // 8 == iota((8, 64), 0)
    bare = [jnp.zeros((n * pack, 64), F32)] * 2
    for kind in range(kinds):
        flat = jnp.dot(base[kind], fan, precision=HIGH, preferred_element_type=F32)
        flat = jnp.sum(jnp.where(mine, flat, 0.0), axis=0, keepdims=True)
        for parity in range(2):
            bare[parity] = jnp.where(kind_of[parity] == kind, flat, bare[parity])
    member = iota((8, 128), 0) == (iota((8, 128), 1) % 64) // 8
    picks = [member & (iota((8, 128), 1) // 64 == parity) for parity in range(2)]

    pl.semaphore_wait(ready, nb - 1)
    total = part[block(me), :].astype(F32)
    for s in range(1, n):
        sends[s - 1].wait_recv()
        total = total + rs_in[s].astype(F32)
    p_all[0] = total.astype(BF)
    gram = lax.dot_general(
        total * weights, total, (((1,), (1,)), ((), ())), precision=HIGH, preferred_element_type=F32
    )
    gram = jnp.where(diagonal, gram, 0.0)
    occ8 = gram[0:8, :]
    for k in range(1, own):
        occ8 = occ8 + gram[k * 8 : k * 8 + 8, :]
    flat = jnp.dot(occ8, spread, precision=HIGH, preferred_element_type=F32)
    flat = jnp.sum(jnp.where(row_of, flat, 0.0), axis=0, keepdims=True)
    for r in range(pack):
        o_in[0, r : r + 1, :] = flat[:, r * 128 : r * 128 + 128]

    def occupancy_copy(q):
        return pltpu.make_async_remote_copy(
            src_ref=o_in.at[0],
            dst_ref=o_in.at[q],
            send_sem=oc_s.at[q],
            recv_sem=oc_r.at[q],
            device_id=place(q),
            device_id_type=MESH,
        )

    each(lambda q: occupancy_copy(q).start())
    p_sends = []
    for s in range(1, n):
        copy = pltpu.make_async_remote_copy(
            src_ref=p_all.at[0],
            dst_ref=p_all.at[s],
            send_sem=ag_s.at[s],
            recv_sem=ag_r.at[s],
            device_id={"pw": lax.rem(me + s, n)},
            device_id_type=MESH,
        )
        copy.start()
        p_sends.append(copy)

    each(lambda q: occupancy_copy(q).wait_recv())
    for d in range(n):
        summed = o_in[d * nb + lax.rem(mb + nb, nb)]
        for b in range(1, nb):
            summed = summed + o_in[d * nb + lax.rem(mb - b + nb, nb)]
        o_sum[d * pack : d * pack + pack, :] = summed
    summed = o_sum[...]
    upper = summed.astype(BF)
    lower = (summed - upper.astype(F32)).astype(BF)
    answer = jnp.dot(
        jnp.concatenate([upper, lower, upper], axis=1), respond[...], preferred_element_type=F32
    )
    matrix = []
    for parity in range(2):
        chosen = jnp.zeros((n * pack, 64), F32)
        for kind in range(kinds):
            at = (parity * kinds + kind) * 64
            chosen = jnp.where(kind_of[parity] == kind, answer[:, at : at + 64], chosen)
        matrix.append(bare[parity] + chosen)
    matrix = jnp.concatenate(matrix, axis=1)
    o_sum[...] = matrix

    for s in range(n):
        lines = []
        for k in range(own):
            at = s * pack + k // 2
            lines.append(
                jnp.where(picks[k % 2], jnp.broadcast_to(o_sum[at : at + 1, :], (8, 128)), 0.0)
            )
        lines = jnp.concatenate(lines, axis=0)
        upper = lines.astype(BF)
        lower = (lines - upper.astype(F32)).astype(BF)
        square = jnp.dot(
            jnp.concatenate([upper, lower], axis=0), gather, preferred_element_type=F32
        )
        upper = jnp.where(diagonal, square[0:rows, :], 0.0)
        lower = jnp.where(diagonal, square[rows : 2 * rows, :], 0.0)
        if s == 0:
            both = upper + lower
            for k in range(own):
                onsite[k] = both[k * 8 : k * 8 + 8, k * 8 : k * 8 + 8]
        if s:
            p_sends[s - 1].wait_recv()
        p = p_all[s]
        w = jnp.dot(
            jnp.concatenate([upper, lower], axis=0).astype(BF), p, preferred_element_type=F32
        )
        w = (w[0:rows, :] + w[rows : 2 * rows, :]).astype(BF)
        owner = lax.rem(me - s + n, n)
        ww[block(owner), :] = w
        second = pl.ds(pl.multiple_of(every + owner * rows, rows), rows)
        ww[second, 0:bands] = -w[:, bands : 2 * bands]
        ww[second, bands : 2 * bands] = w[:, 0:bands]
    result = jnp.dot(beta_t[...], ww[...], preferred_element_type=F32).astype(BF)
    applied[0] = result[:, 0:bands]
    applied[1] = result[:, bands : 2 * bands]
    for copy in sends + p_sends:
        copy.wait_send()
    each(lambda q: occupancy_copy(q).wait_send())


def finish(applied_in, onsite_in, applied, onsite, sem):
    copies = [
        pltpu.make_async_copy(applied_in, applied, sem.at[0]),
        pltpu.make_async_copy(onsite_in, onsite, sem.at[1]),
    ]
    for copy in copies:
        copy.start()
    for copy in copies:
        copy.wait()


def solution(mesh):
    n, nb = mesh.shape["pw"], mesh.shape["band"]

    def local(wave, miller, reciprocal, fractional, species, order, widths, base, coupling, occ):
        _, npw, bands = wave.shape
        atoms = order.shape[0]
        own = atoms // n
        rows, every = own * 8, atoms * 8
        pack = own // 2
        kinds = widths.shape[0]
        vmem = pl.BlockSpec(memory_space=pltpu.VMEM)
        hbm = pl.BlockSpec(memory_space=pltpu.HBM)
        dma = pltpu.SemaphoreType.DMA
        results = (
            jax.ShapeDtypeStruct(wave.shape, BF),
            jax.ShapeDtypeStruct((own, 8, 8), F32),
        )
        first = pl.pallas_call(
            functools.partial(kernel, n, nb),
            out_shape=results,
            in_specs=[hbm] * 10,
            out_specs=(vmem, vmem),
            scratch_shapes=[
                pltpu.VMEM(miller.shape, jnp.int32),
                pltpu.SMEM(reciprocal.shape, F32),
                pltpu.SMEM(fractional.shape, F32),
                pltpu.SMEM(species.shape, jnp.int32),
                pltpu.SMEM(order.shape, jnp.int32),
                pltpu.SMEM(widths.shape, F32),
                pltpu.VMEM(base.shape, F32),
                pltpu.VMEM(coupling.shape, F32),
                pltpu.VMEM((1, bands), F32),
                pltpu.VMEM((2 * npw, 2 * bands), BF),
                pltpu.VMEM((atoms, npw), F32),
                pltpu.VMEM((atoms, npw), F32),
                pltpu.VMEM((atoms, npw), F32),
                pltpu.VMEM((kinds, 8, npw), F32),
                pltpu.VMEM((every, 2 * npw), BF),
                pltpu.VMEM((npw, 2 * every), BF),
                pltpu.VMEM((every, 2 * bands), BF),
                pltpu.VMEM((n, rows, 2 * bands), BF),
                pltpu.VMEM((n, rows, 2 * bands), BF),
                pltpu.VMEM((n * nb, pack, 128), F32),
                pltpu.VMEM((n * pack, 128), F32),
                pltpu.VMEM((384, kinds * 128), BF),
                pltpu.VMEM((2 * every, 2 * bands), BF),
                dma((12,)),
                dma((n,)),
                dma((n,)),
                dma((n,)),
                dma((n,)),
                dma((n * nb,)),
                dma((n * nb,)),
                pltpu.SemaphoreType.REGULAR,
            ],
            compiler_params=pltpu.CompilerParams(
                collective_id=0, has_side_effects=True, vmem_limit_bytes=40 * 2**20
            ),
        )(
            *[
                pltpu.with_memory_space_constraint(value, pltpu.HBM)
                for value in (
                    wave,
                    miller,
                    reciprocal,
                    fractional,
                    species,
                    order,
                    widths,
                    base,
                    coupling,
                    occ.reshape(1, bands),
                )
            ]
        )
        anywhere = pl.BlockSpec(memory_space=pl.ANY)
        return pl.pallas_call(
            finish,
            out_shape=results,
            in_specs=[anywhere] * 2,
            out_specs=(hbm, hbm),
            scratch_shapes=[dma((2,))],
            compiler_params=pltpu.CompilerParams(vmem_limit_bytes=2**20),
        )(*first)

    placed = (P(None, "pw", "band"), P(None, "pw"), P(), P(), P(), P(), P(), P(), P(), P("band"))
    return jax.shard_map(
        local,
        mesh=mesh,
        in_specs=placed,
        out_specs=(P(None, "pw", "band"), P("pw", None, None)),
        check_vma=False,
    )
```

profile of v0, /device:TPU:0, one launch (start us, length us, event | category | flops | bytes accessed | tf_op | source)
XLA Modules:
  0.0 19.5 jit_solution(11002672874570427936)
XLA Ops:
  0.6 18.2 %shard_map.113 = (bf16[2,512,128]{2,1,0:T(8,128)(2,1)S(1)}, f32[4,8,8]{2,1,0:T(8,128)S(1)}) custom-call(bf16[2,512,128]{2,1,0:T(8,128)(2,1)} %wave.1, s32[3,512]{1,0:T(4,128)} %miller_h.1, f32[3,3]{1,0:T(4,128)} %reciprocal_h.1, f32[3,32]{1,0:T(4,128)} %fractional_h.1, s32[32]{0:T(128)} %species_h.1, s32[32]{0:T(128)} %order_h.1, f32[4,4]{1,0:T(4,128)} %widths_h.1, ...), custom_call_target="tpu_custom_call" | custom-call | tf_op jit(solution)/shard_map/pallas_call | solution.py:394
  18.8 0.7 %shard_map.114 = (bf16[2,512,128]{2,1,0:T(8,128)(2,1)}, f32[4,8,8]{2,1,0:T(8,128)}) custom-call(bf16[2,512,128]{2,1,0:T(8,128)(2,1)S(1)} %get-tuple-element.4.applied_in, f32[4,8,8]{2,1,0:T(8,128)S(1)} %get-tuple-element.5.onsite_in), custom_call_target="tpu_custom_call" | custom-call | tf_op jit(solution)/shard_map/pallas_call | solution.py:453
where the time goes:
time: 19.8 us; the launch traced here: 19.5 us
  Pallas kernels  18.9 us (95%)
  between operations  0.64 us (3%)
    pallas_call x1, Pallas kernels, local(): pl.pallas_call(functools.partial(kernel, n, nb), out_shape=results, in_sp...  18.2 us
    pallas_call x1, Pallas kernels, local(): pl.pallas_call(finish, out_shape=results, in_specs=[anywhere] * 2, out_sp...  0.72 us

commit v1 on v0

--- a/solution.py
+++ b/solution.py
@@ -72,7 +72,12 @@
     p_all,
     o_in,
     o_sum,
+    spread,
+    turned,
+    respond_t,
     respond,
+    bare,
+    folded,
     ww,
     load_sem,
     rs_s,
@@ -90,7 +95,6 @@
     atoms = order.shape[0]
     kinds = widths.shape[0]
     own = atoms // n
-    pack = own // 2
     rows = own * 8
     every = atoms * 8
     peers = n * nb
@@ -116,16 +120,6 @@
         copy.start()
     barrier = pltpu.get_barrier_semaphore()
 
-    def place(q):
-        return {"pw": lax.rem(me + q // nb, n), "band": lax.rem(mb + lax.rem(q, nb), nb)}
-
-    def each(step):
-        if peers <= 64:
-            for q in range(1, peers):
-                step(q)
-        else:
-            lax.fori_loop(1, peers, lambda q, carry: (step(q), carry)[1], 0)
-
     for d in range(1, n):
         pl.semaphore_signal(
             barrier, inc=1, device_id={"pw": lax.rem(me + d, n)}, device_id_type=MESH
@@ -226,141 +220,144 @@
     beta_t[:, every : 2 * every] = beta[:, npw : 2 * npw].T
     weights = occ[...] * (1.0 / (bands * nb))
     weights = jnp.concatenate([weights, weights], axis=1)
-    spread = (
-        (iota((rows, own * 64), 0) // 8 == iota((rows, own * 64), 1) // 64)
-        & (iota((rows, own * 64), 0) % 8 == iota((rows, own * 64), 1) % 8)
-    ).astype(F32)
-    row_of = (iota((8, own * 64), 1) % 64) // 8 == iota((8, own * 64), 0)
-    diagonal = iota((rows, rows), 0) // 8 == iota((rows, rows), 1) // 8
-    gather = (iota((128, rows), 0) % 8 == iota((128, rows), 1) % 8).astype(BF)
-    flipped = coupling[...].reshape(kinds * 64, 64).T
-    upper = flipped.astype(BF)
-    lower = (flipped - upper.astype(F32)).astype(BF)
-    none = jnp.zeros_like(upper)
-    for i, piece in enumerate((upper, upper, lower)):
-        respond[i * 128 : i * 128 + 64, :] = jnp.concatenate([piece, none], axis=1)
-        respond[i * 128 + 64 : i * 128 + 128, :] = jnp.concatenate([none, piece], axis=1)
-    line = iota((n * pack, 64), 0)
-    kind_of = []
-    for parity in range(2):
-        column = jnp.zeros((n * pack, 64), jnp.int32)
-        for row in range(n * pack):
-            owner = lax.rem(me - row // pack + n, n)
-            kind = species[order[owner * own + (row % pack) * 2 + parity]]
-            column = jnp.where(line == row, kind, column)
-        kind_of.append(column)
-    fan = (iota((8, 64), 1) % 8 == iota((8, 64), 0)).astype(F32)
-    mine = iota((8, 64), 1) // 8 == iota((8, 64), 0)
-    bare = [jnp.zeros((n * pack, 64), F32)] * 2
+    group = min(atoms, 32)
+    span = group * 8
+    fan = (iota((8, span), 1) % 8 == iota((8, span), 0)).astype(F32)
+    diagonal = iota((span, span), 0) // 8 == iota((span, span), 1) // 8
+    fold = (iota((span, 8), 0) % 8 == iota((span, 8), 1)).astype(F32)
+    slot = [iota((8, 128), 0) == 2 * t + iota((8, 128), 1) // 64 for t in range(4)]
     for kind in range(kinds):
-        flat = jnp.dot(base[kind], fan, precision=HIGH, preferred_element_type=F32)
-        flat = jnp.sum(jnp.where(mine, flat, 0.0), axis=0, keepdims=True)
-        for parity in range(2):
-            bare[parity] = jnp.where(kind_of[parity] == kind, flat, bare[parity])
-    member = iota((8, 128), 0) == (iota((8, 128), 1) % 64) // 8
-    picks = [member & (iota((8, 128), 1) // 64 == parity) for parity in range(2)]
+        spread[kind] = jnp.dot(base[kind], fan, precision=HIGH, preferred_element_type=F32)
+        for t in range(4):
+            turned[kind, :, t * 128 : t * 128 + 128] = jnp.concatenate(
+                [coupling[kind, i * 8 : i * 8 + 8, :] for i in (2 * t, 2 * t + 1)], axis=1
+            )
+
+    def expand(pair, carry):
+        kind = [species[order[pair * 2 + e]] for e in range(2)]
+        at = pl.ds(pl.multiple_of(pair * 16, 16), 16)
+        respond_t[at, :] = jnp.concatenate([turned[s] for s in kind], axis=0).astype(BF)
+        bare[at, :] = jnp.concatenate([spread[s] for s in kind], axis=0)
+        return carry
+
+    lax.fori_loop(0, atoms // 2, expand, 0, unroll=4)
+    for q in range(0, every, span):
+        respond[:, q : q + span] = respond_t[q : q + span, :].T
 
     pl.semaphore_wait(ready, nb - 1)
     total = part[block(me), :].astype(F32)
     for s in range(1, n):
         sends[s - 1].wait_recv()
         total = total + rs_in[s].astype(F32)
-    p_all[0] = total.astype(BF)
-    gram = lax.dot_general(
-        total * weights, total, (((1,), (1,)), ((), ())), precision=HIGH, preferred_element_type=F32
+    p_all[block(me), :] = total.astype(BF)
+    pairs = []
+    for k in range(own):
+        left = total[k * 8 : k * 8 + 8, :] * weights
+        pair = jnp.concatenate(
+            [jnp.broadcast_to(total[k * 8 + i : k * 8 + i + 1, :], (8, 2 * bands)) * left for i in range(8)], axis=0
+        ).astype(BF)
+        pairs += [pair, pair]
+    flat = lax.dot_general(
+        jnp.ones((16, 2 * bands), BF),
+        jnp.concatenate(pairs, axis=0),
+        (((1,), (1,)), ((), ())),
+        preferred_element_type=F32,
     )
-    gram = jnp.where(diagonal, gram, 0.0)
-    occ8 = gram[0:8, :]
-    for k in range(1, own):
-        occ8 = occ8 + gram[k * 8 : k * 8 + 8, :]
-    flat = jnp.dot(occ8, spread, precision=HIGH, preferred_element_type=F32)
-    flat = jnp.sum(jnp.where(row_of, flat, 0.0), axis=0, keepdims=True)
-    for r in range(pack):
-        o_in[0, r : r + 1, :] = flat[:, r * 128 : r * 128 + 128]
-
-    def occupancy_copy(q):
+    for k in range(own):
+        o_in[mb, me, k : k + 1, :] = flat[0:1, k * 128 : k * 128 + 128]
+
+    def skip(i, at, size):
+        return i + (i + size - at) // size
+
+    def occupancy_copy(to, band, by_owner, by_band, at):
         return pltpu.make_async_remote_copy(
-            src_ref=o_in.at[0],
-            dst_ref=o_in.at[q],
-            send_sem=oc_s.at[q],
-            recv_sem=oc_r.at[q],
-            device_id=place(q),
+            src_ref=o_in.at[mb, me],
+            dst_ref=o_in.at[mb, me],
+            send_sem=oc_s.at[at],
+            recv_sem=oc_r.at[by_owner * nb + by_band],
+            device_id={"pw": to, "band": band},
             device_id_type=MESH,
         )
 
-    each(lambda q: occupancy_copy(q).start())
+    def away(i, j):
+        return skip(i, me, n), j
+
+    def near(j):
+        return me, skip(j, mb, nb)
+
+    def each_peer(step):
+        if peers <= 64:
+            for i in range(n - 1):
+                for j in range(nb):
+                    step(*away(i, j), i * nb + j)
+        else:
+            lax.fori_loop(
+                0, (n - 1) * nb, lambda q, c: (step(*away(q // nb, lax.rem(q, nb)), q), c)[1], 0
+            )
+        for j in range(nb - 1):
+            step(*near(j), (n - 1) * nb + j)
+
+    each_peer(lambda to, band, at: occupancy_copy(to, band, me, mb, at).start())
     p_sends = []
-    for s in range(1, n):
+    for i in range(n - 1):
+        to = skip(i, me, n)
         copy = pltpu.make_async_remote_copy(
-            src_ref=p_all.at[0],
-            dst_ref=p_all.at[s],
-            send_sem=ag_s.at[s],
-            recv_sem=ag_r.at[s],
-            device_id={"pw": lax.rem(me + s, n)},
+            src_ref=p_all.at[block(me)],
+            dst_ref=p_all.at[block(me)],
+            send_sem=ag_s.at[i],
+            recv_sem=ag_r.at[me],
+            device_id={"pw": to},
             device_id_type=MESH,
         )
         copy.start()
         p_sends.append(copy)
 
-    each(lambda q: occupancy_copy(q).wait_recv())
+    each_peer(lambda to, band, at: occupancy_copy(to, band, to, band, at).wait_recv())
     for d in range(n):
-        summed = o_in[d * nb + lax.rem(mb + nb, nb)]
+        summed = o_in[0, d]
         for b in range(1, nb):
-            summed = summed + o_in[d * nb + lax.rem(mb - b + nb, nb)]
-        o_sum[d * pack : d * pack + pack, :] = summed
-    summed = o_sum[...]
-    upper = summed.astype(BF)
-    lower = (summed - upper.astype(F32)).astype(BF)
-    answer = jnp.dot(
-        jnp.concatenate([upper, lower, upper], axis=1), respond[...], preferred_element_type=F32
-    )
+            summed = summed + o_in[b, d]
+        o_sum[d * own : d * own + own, :] = summed
     matrix = []
-    for parity in range(2):
-        chosen = jnp.zeros((n * pack, 64), F32)
-        for kind in range(kinds):
-            at = (parity * kinds + kind) * 64
-            chosen = jnp.where(kind_of[parity] == kind, answer[:, at : at + 64], chosen)
-        matrix.append(bare[parity] + chosen)
-    matrix = jnp.concatenate(matrix, axis=1)
-    o_sum[...] = matrix
-
-    for s in range(n):
+    for q in range(0, atoms, group):
         lines = []
-        for k in range(own):
-            at = s * pack + k // 2
+        for k in range(q, q + group):
+            line = jnp.broadcast_to(o_sum[k : k + 1, :], (8, 128))
             lines.append(
-                jnp.where(picks[k % 2], jnp.broadcast_to(o_sum[at : at + 1, :], (8, 128)), 0.0)
+                jnp.concatenate([jnp.where(slot[t], line, 0.0) for t in range(4)], axis=1)
             )
-        lines = jnp.concatenate(lines, axis=0)
-        upper = lines.astype(BF)
-        lower = (lines - upper.astype(F32)).astype(BF)
-        square = jnp.dot(
-            jnp.concatenate([upper, lower], axis=0), gather, preferred_element_type=F32
-        )
-        upper = jnp.where(diagonal, square[0:rows, :], 0.0)
-        lower = jnp.where(diagonal, square[rows : 2 * rows, :], 0.0)
-        if s == 0:
-            both = upper + lower
-            for k in range(own):
-                onsite[k] = both[k * 8 : k * 8 + 8, k * 8 : k * 8 + 8]
-        if s:
-            p_sends[s - 1].wait_recv()
-        p = p_all[s]
-        w = jnp.dot(
-            jnp.concatenate([upper, lower], axis=0).astype(BF), p, preferred_element_type=F32
-        )
-        w = (w[0:rows, :] + w[rows : 2 * rows, :]).astype(BF)
-        owner = lax.rem(me - s + n, n)
-        ww[block(owner), :] = w
-        second = pl.ds(pl.multiple_of(every + owner * rows, rows), rows)
-        ww[second, 0:bands] = -w[:, bands : 2 * bands]
-        ww[second, bands : 2 * bands] = w[:, 0:bands]
+        lines = jnp.concatenate(lines, axis=0).astype(BF)
+        answer = jnp.dot(
+            lines, respond[:, q * 8 : q * 8 + span], preferred_element_type=F32
+        )
+        answer = jnp.where(diagonal, answer + bare[q * 8 : q * 8 + span, :], 0.0)
+        folded[q * 8 : q * 8 + span, :] = answer
+        matrix.append(answer.astype(BF))
+    for s in range(1, n):
+        owner = lax.rem(me + s, n)
+        pltpu.make_async_remote_copy(
+            src_ref=p_all.at[block(owner)],
+            dst_ref=p_all.at[block(owner)],
+            send_sem=ag_s.at[0],
+            recv_sem=ag_r.at[owner],
+            device_id={"pw": owner},
+            device_id_type=MESH,
+        ).wait_recv()
+    for q in range(0, every, span):
+        w = jnp.dot(matrix[q // span], p_all[q : q + span, :], preferred_element_type=F32)
+        w = w.astype(BF)
+        ww[q : q + span, :] = w
+        ww[every + q : every + q + span, 0:bands] = -w[:, bands : 2 * bands]
+        ww[every + q : every + q + span, bands : 2 * bands] = w[:, 0:bands]
     result = jnp.dot(beta_t[...], ww[...], preferred_element_type=F32).astype(BF)
     applied[0] = result[:, 0:bands]
     applied[1] = result[:, bands : 2 * bands]
+    mine = jnp.dot(folded[block(me), :], fold, precision=HIGH, preferred_element_type=F32)
+    for k in range(own):
+        onsite[k] = mine[k * 8 : k * 8 + 8, :]
     for copy in sends + p_sends:
         copy.wait_send()
-    each(lambda q: occupancy_copy(q).wait_send())
+    each_peer(lambda to, band, at: occupancy_copy(to, band, me, mb, at).wait_send())
 
 
 def finish(applied_in, onsite_in, applied, onsite, sem):
@@ -382,7 +379,7 @@
         atoms = order.shape[0]
         own = atoms // n
         rows, every = own * 8, atoms * 8
-        pack = own // 2
+        span = min(atoms, 32) * 8
         kinds = widths.shape[0]
         vmem = pl.BlockSpec(memory_space=pltpu.VMEM)
         hbm = pl.BlockSpec(memory_space=pltpu.HBM)
@@ -415,10 +412,15 @@
                 pltpu.VMEM((npw, 2 * every), BF),
                 pltpu.VMEM((every, 2 * bands), BF),
                 pltpu.VMEM((n, rows, 2 * bands), BF),
-                pltpu.VMEM((n, rows, 2 * bands), BF),
-                pltpu.VMEM((n * nb, pack, 128), F32),
-                pltpu.VMEM((n * pack, 128), F32),
-                pltpu.VMEM((384, kinds * 128), BF),
+                pltpu.VMEM((every, 2 * bands), BF),
+                pltpu.VMEM((nb, n, own, 128), F32),
+                pltpu.VMEM((atoms, 128), F32),
+                pltpu.VMEM((kinds, 8, span), F32),
+                pltpu.VMEM((kinds, 8, 512), F32),
+                pltpu.VMEM((every, 512), BF),
+                pltpu.VMEM((512, every), BF),
+                pltpu.VMEM((every, span), F32),
+                pltpu.VMEM((every, span), F32),
                 pltpu.VMEM((2 * every, 2 * bands), BF),
                 dma((12,)),
                 dma((n,)),

time: 19.8 us -> 18.6 us (0.939)
  Pallas kernels: 18.9 us -> 17.7 us
    pallas_call x1, Pallas kernels: 18.2 us -> 17 us  [local(): pl.pallas_call(functools.partial(kernel, n, nb), out_shape=results, in_sp...]
where the time goes in v1:
time: 18.6 us; the launch traced here: 18.4 us
  Pallas kernels  17.7 us (95%)
  between operations  0.64 us (3%)
    pallas_call x1, Pallas kernels, local(): pl.pallas_call(functools.partial(kernel, n, nb), out_shape=results, in_sp...  17 us
    pallas_call x1, Pallas kernels, local(): pl.pallas_call(finish, out_shape=results, in_specs=[anywhere] * 2, out_sp...  0.72 us

profile of v1, /device:TPU:0, one launch (start us, length us, event | category | flops | bytes accessed | tf_op | source)
XLA Modules:
  0.0 18.4 jit_solution(6489947752093624808)
XLA Ops:
  0.6 17.0 %shard_map.113 = (bf16[2,512,128]{2,1,0:T(8,128)(2,1)S(1)}, f32[4,8,8]{2,1,0:T(8,128)S(1)}) custom-call(bf16[2,512,128]{2,1,0:T(8,128)(2,1)} %wave.1, s32[3,512]{1,0:T(4,128)} %miller_h.1, f32[3,3]{1,0:T(4,128)} %reciprocal_h.1, f32[3,32]{1,0:T(4,128)} %fractional_h.1, s32[32]{0:T(128)} %species_h.1, s32[32]{0:T(128)} %order_h.1, f32[4,4]{1,0:T(4,128)} %widths_h.1, ...), custom_call_target="tpu_custom_call" | custom-call | tf_op jit(solution)/shard_map/pallas_call | solution.py:391
  17.7 0.7 %shard_map.114 = (bf16[2,512,128]{2,1,0:T(8,128)(2,1)}, f32[4,8,8]{2,1,0:T(8,128)}) custom-call(bf16[2,512,128]{2,1,0:T(8,128)(2,1)S(1)} %get-tuple-element.4.applied_in, f32[4,8,8]{2,1,0:T(8,128)S(1)} %get-tuple-element.5.onsite_in), custom_call_target="tpu_custom_call" | custom-call | tf_op jit(solution)/shard_map/pallas_call | solution.py:455

commit v2 on v1

--- a/solution.py
+++ b/solution.py
@@ -68,6 +68,9 @@
     beta,
     beta_t,
     part,
+    kept,
+    pair_in,
+    pair_sum,
     rs_in,
     p_all,
     o_in,
@@ -80,6 +83,8 @@
     folded,
     ww,
     load_sem,
+    sw_s,
+    sw_r,
     rs_s,
     rs_r,
     ag_s,
@@ -87,6 +92,9 @@
     oc_s,
     oc_r,
     ready,
+    here,
+    here_b,
+    go,
 ):
     me = lax.axis_index("pw")
     mb = lax.axis_index("band")
@@ -98,6 +106,21 @@
     rows = own * 8
     every = atoms * 8
     peers = n * nb
+    chips = n // 2
+    half = chips * rows
+    chip, side = me // 2, lax.rem(me, 2)
+    mate = me + 1 - 2 * side
+    single, double = chips // 2, chips // 4
+    chunk = 2 * rows
+
+    def handled(z):
+        return 1 if z < single else 2 if z < single + double else 0
+
+    def first_slot(z):
+        return z if z < single else 2 * z - single
+
+    def atom_at(k):
+        return order[(2 * (k // own % chips) + k // own // chips) * own + k % own]
 
     small = [
         (miller_h, miller),
@@ -119,15 +142,38 @@
     for copy in loads:
         copy.start()
     barrier = pltpu.get_barrier_semaphore()
-
-    for d in range(1, n):
-        pl.semaphore_signal(
-            barrier, inc=1, device_id={"pw": lax.rem(me + d, n)}, device_id_type=MESH
-        )
-    for b in range(1, nb):
-        pl.semaphore_signal(
-            barrier, inc=1, device_id={"band": lax.rem(mb + b, nb)}, device_id_type=MESH
-        )
+    others = [lax.rem(me + d, n) for d in range(1, n)]
+    group_bands = [lax.rem(mb + d, nb) for d in range(1, nb)]
+
+    hub = n // 2 - 1
+
+    def greet(sem, later):
+        for to in others:
+            @pl.when(to > me if later else to < me)
+            def _():
+                pl.semaphore_signal(
+                    sem(0), inc=1, device_id={"pw": to}, device_id_type=MESH
+                )
+
+        @pl.when(me == hub)
+        def _():
+            for to in group_bands:
+                @pl.when(to > mb if later else to < mb)
+                def _():
+                    pl.semaphore_signal(
+                        sem(1), inc=1, device_id={"band": to}, device_id_type=MESH
+                    )
+
+    greet(lambda axis: barrier, True)
+    @pl.when(jnp.logical_and(me > 0, me != hub))
+    def _():
+        pl.semaphore_wait(barrier, me)
+
+    @pl.when(me == hub)
+    def _():
+        pl.semaphore_wait(barrier, hub + mb)
+
+    greet(lambda axis: here_b if axis else here.at[me], False)
     for copy in loads[0:6]:
         copy.wait()
 
@@ -144,77 +190,97 @@
     factor = jnp.where(
         (j == 2) | (j == 5), wide[0], jnp.where((j == 3) | (j == 6), wide[1], wide[2])
     )
-    half = jnp.broadcast_to(-0.5 * g2, (8, npw))
+    decay = jnp.broadcast_to(-0.5 * g2, (8, npw))
     for s in range(widths.shape[0]):
         w = jnp.where(
             j == 0,
             widths[s, 0],
             jnp.where(j == 1, widths[s, 1], jnp.where(j < 5, widths[s, 2], widths[s, 3])),
         )
-        amp[s] = jnp.where(is_s, 1.0, factor * w) * jnp.exp(half * (w * w))
-
-    def position(k, carry):
-        a = order[k]
-        xs[pl.ds(k, 1), :] = (
-            fractional[0, a] * m[0] + fractional[1, a] * m[1] + fractional[2, a] * m[2]
-        )
-        return carry
-
-    lax.fori_loop(0, atoms, position, 0, unroll=8)
-    x = xs[...]
-    t = x - jnp.round(x)
-    u = t * t
-    cs[...] = series(COS, u)
-    sn[...] = t * series(SIN, u)
-
-    def projector(pair, carry):
-        real, imag = [], []
-        for e in range(2):
-            k = pair * 2 + e
-            c = jnp.broadcast_to(cs[pl.ds(k, 1), :], (8, npw))
-            s = jnp.broadcast_to(sn[pl.ds(k, 1), :], (8, npw))
-            a = amp[species[order[k]]]
-            real.append(a * jnp.where(is_s, c, -s))
-            imag.append(-a * jnp.where(is_s, s, c))
-        at = pl.ds(pl.multiple_of(pair * 16, 16), 16)
-        beta[at, 0:npw] = jnp.concatenate(real, axis=0).astype(BF)
-        beta[at, npw : 2 * npw] = jnp.concatenate(imag, axis=0).astype(BF)
-        return carry
-
-    lax.fori_loop(0, atoms // 2, projector, 0, unroll=4)
-
+        amp[s] = jnp.where(is_s, 1.0, factor * w) * jnp.exp(decay * (w * w))
+
+    def at_row(start, size):
+        return pl.ds(pl.multiple_of(start, rows), size)
+
+    def scatter(z):
+        size = handled(z) * rows
+        return pltpu.make_async_remote_copy(
+            src_ref=pair_sum.at[pl.ds(first_slot(z) * rows, size)],
+            dst_ref=rs_in.at[chip, pl.ds(0, size)],
+            send_sem=rs_s.at[z],
+            recv_sem=rs_r.at[chip],
+            device_id={"pw": 2 * z + side},
+            device_id_type=MESH,
+        )
+
+    def swap(c):
+        return pltpu.make_async_remote_copy(
+            src_ref=part.at[pl.ds(c, chunk)],
+            dst_ref=pair_in.at[pl.ds(c, chunk)],
+            send_sem=sw_s.at[c // chunk],
+            recv_sem=sw_r.at[c // chunk],
+            device_id={"pw": mate},
+            device_id_type=MESH,
+        )
+
+    def projectors(which, c):
+        first = (c // rows) * 2 * own + which * own
+        at = c // 8
+        atom = [
+            order[first + (k // own) * 2 * own + k % own] for k in range(chunk // 8)
+        ]
+        for k, a in enumerate(atom):
+            xs[at + k : at + k + 1, :] = (
+                fractional[0, a] * m[0] + fractional[1, a] * m[1] + fractional[2, a] * m[2]
+            )
+        x = xs[at : at + chunk // 8, :]
+        t = x - jnp.round(x)
+        u = t * t
+        cs[at : at + chunk // 8, :] = series(COS, u)
+        sn[at : at + chunk // 8, :] = t * series(SIN, u)
+        for pair in range(chunk // 16):
+            real, imag = [], []
+            for k in (2 * pair, 2 * pair + 1):
+                c_k = jnp.broadcast_to(cs[at + k : at + k + 1, :], (8, npw))
+                s_k = jnp.broadcast_to(sn[at + k : at + k + 1, :], (8, npw))
+                a_k = amp[species[atom[k]]]
+                real.append(a_k * jnp.where(is_s, c_k, -s_k))
+                imag.append(-a_k * jnp.where(is_s, s_k, c_k))
+            to = pl.ds(pl.multiple_of(which * half + c + pair * 16, 16), 16)
+            beta[to, 0:npw] = jnp.concatenate(real, axis=0).astype(BF)
+            beta[to, npw : 2 * npw] = jnp.concatenate(imag, axis=0).astype(BF)
+
+    steps = [(1 - side, c, True) for c in range(0, half, chunk)]
+    steps += [(side, c, False) for c in range(0, half, chunk)]
+    projectors(*steps[0][:2])
     for copy in loads[6:]:
         copy.wait()
     wv[npw : 2 * npw, bands : 2 * bands] = -wv[0:npw, 0:bands]
-    part[...] = jnp.dot(beta[...], wv[...], preferred_element_type=F32).astype(BF)
-    pl.semaphore_wait(barrier, n - 1 + nb - 1)
-
-    def block(index):
-        return pl.ds(pl.multiple_of(index * rows, rows), rows)
-
-    def scatter(s):
-        to = lax.rem(me + s, n)
-        return pltpu.make_async_remote_copy(
-            src_ref=part.at[block(to)],
-            dst_ref=rs_in.at[s],
-            send_sem=rs_s.at[s],
-            recv_sem=rs_r.at[s],
-            device_id={"pw": to},
-            device_id_type=MESH,
-        )
-
-    upper_half = me // (n // 2)
-    far_first = [
-        lax.rem(n - 2 - me + upper_half + (2 * upper_half - 1) * i + 2 * (n - 1), n - 1) + 1
-        for i in range(n - 1)
-    ]
-    sends = [scatter(s) for s in range(1, n)]
-    for s in far_first:
-        scatter(s).start()
-    for b in range(1, nb):
-        pl.semaphore_signal(
-            ready, inc=1, device_id={"band": lax.rem(mb + b, nb)}, device_id_type=MESH
-        )
+    for index, (which, c, away) in enumerate(steps):
+        value = jnp.dot(
+            beta[at_row(which * half + c, chunk), :], wv[...], preferred_element_type=F32
+        )
+        if index + 1 < len(steps):
+            projectors(*steps[index + 1][:2])
+        if away:
+            part[c : c + chunk, :] = value.astype(BF)
+            if index == 0:
+                @pl.when(side == 0)
+                def _():
+                    pl.semaphore_wait(here.at[mate], 1)
+            swap(c).start()
+        else:
+            kept[c : c + chunk, :] = value
+    for c in range(0, half, chunk):
+        swap(c).wait_recv()
+        pair_sum[c : c + chunk, :] = (
+            kept[c : c + chunk, :] + pair_in[c : c + chunk, :].astype(F32)
+        ).astype(BF)
+        for z in range(single + double):
+            if c <= first_slot(z) * rows < c + chunk:
+                @pl.when(z < chip)
+                def _():
+                    scatter(z).start()
 
     beta_t[:, 0:every] = beta[:, 0:npw].T
     beta_t[:, every : 2 * every] = beta[:, npw : 2 * npw].T
@@ -233,48 +299,46 @@
                 [coupling[kind, i * 8 : i * 8 + 8, :] for i in (2 * t, 2 * t + 1)], axis=1
             )
 
-    def expand(pair, carry):
-        kind = [species[order[pair * 2 + e]] for e in range(2)]
-        at = pl.ds(pl.multiple_of(pair * 16, 16), 16)
-        respond_t[at, :] = jnp.concatenate([turned[s] for s in kind], axis=0).astype(BF)
-        bare[at, :] = jnp.concatenate([spread[s] for s in kind], axis=0)
-        return carry
-
-    lax.fori_loop(0, atoms // 2, expand, 0, unroll=4)
+    for k in range(0, atoms, 2):
+        kind = [species[atom_at(k + e)] for e in range(2)]
+        respond_t[k * 8 : k * 8 + 16, :] = jnp.concatenate(
+            [turned[s] for s in kind], axis=0
+        ).astype(BF)
+        bare[k * 8 : k * 8 + 16, :] = jnp.concatenate([spread[s] for s in kind], axis=0)
     for q in range(0, every, span):
         respond[:, q : q + span] = respond_t[q : q + span, :].T
 
-    pl.semaphore_wait(ready, nb - 1)
-    total = part[block(me), :].astype(F32)
-    for s in range(1, n):
-        sends[s - 1].wait_recv()
-        total = total + rs_in[s].astype(F32)
-    p_all[block(me), :] = total.astype(BF)
-    pairs = []
-    for k in range(own):
-        left = total[k * 8 : k * 8 + 8, :] * weights
-        pair = jnp.concatenate(
-            [jnp.broadcast_to(total[k * 8 + i : k * 8 + i + 1, :], (8, 2 * bands)) * left for i in range(8)], axis=0
-        ).astype(BF)
-        pairs += [pair, pair]
-    flat = lax.dot_general(
-        jnp.ones((16, 2 * bands), BF),
-        jnp.concatenate(pairs, axis=0),
-        (((1,), (1,)), ((), ())),
-        preferred_element_type=F32,
-    )
-    for k in range(own):
-        o_in[mb, me, k : k + 1, :] = flat[0:1, k * 128 : k * 128 + 128]
+    for to in range(1, n):
+        @pl.when(jnp.logical_and(to > me, to != mate))
+        def _():
+            pl.semaphore_wait(here.at[to], 1)
+
+        if to // 2 < single + double:
+            @pl.when(jnp.logical_and(to // 2 > chip, to % 2 == side))
+            def _():
+                scatter(to // 2).start()
+
+    @pl.when(me == hub)
+    def _():
+        @pl.when(mb < nb - 1)
+        def _():
+            pl.semaphore_wait(here_b, nb - 1 - mb)
+
+        for to in group_bands:
+            pl.semaphore_signal(ready, inc=1, device_id={"band": to}, device_id_type=MESH)
+        pl.semaphore_wait(ready, nb - 1)
+        for to in others:
+            pl.semaphore_signal(go, inc=1, device_id={"pw": to}, device_id_type=MESH)
 
     def skip(i, at, size):
         return i + (i + size - at) // size
 
-    def occupancy_copy(to, band, by_owner, by_band, at):
+    def occupancy_copy(to, band, at, first, count):
         return pltpu.make_async_remote_copy(
-            src_ref=o_in.at[mb, me],
-            dst_ref=o_in.at[mb, me],
+            src_ref=o_in.at[pl.ds(mb * n + first, count)],
+            dst_ref=o_in.at[pl.ds(mb * n + first, count)],
             send_sem=oc_s.at[at],
-            recv_sem=oc_r.at[by_owner * nb + by_band],
+            recv_sem=oc_r,
             device_id={"pw": to, "band": band},
             device_id_type=MESH,
         )
@@ -297,26 +361,100 @@
         for j in range(nb - 1):
             step(*near(j), (n - 1) * nb + j)
 
-    each_peer(lambda to, band, at: occupancy_copy(to, band, me, mb, at).start())
-    p_sends = []
-    for i in range(n - 1):
-        to = skip(i, me, n)
-        copy = pltpu.make_async_remote_copy(
-            src_ref=p_all.at[block(me)],
-            dst_ref=p_all.at[block(me)],
+    def projection_copy(i, first, count):
+        at = at_row(first * rows, count * rows)
+        return pltpu.make_async_remote_copy(
+            src_ref=p_all.at[at],
+            dst_ref=p_all.at[at],
             send_sem=ag_s.at[i],
-            recv_sem=ag_r.at[me],
-            device_id={"pw": to},
+            recv_sem=ag_r,
+            device_id={"pw": skip(i, me, n)},
             device_id_type=MESH,
         )
-        copy.start()
-        p_sends.append(copy)
-
-    each_peer(lambda to, band, at: occupancy_copy(to, band, to, band, at).wait_recv())
+
+    def own_first(count):
+        return side * chips + (chip if count == 1 else 2 * chip - single)
+
+    def each_role(act):
+        for count, role in (
+            (1, chip < single),
+            (2, jnp.logical_and(chip >= single, chip < single + double)),
+            (0, chip >= single + double),
+        ):
+            @pl.when(role)
+            def _():
+                act(count)
+
+    def wait_go():
+        @pl.when(me != hub)
+        def _():
+            pl.semaphore_wait(go, 1)
+
+    def share(count):
+        if count == 0:
+            wait_go()
+            return
+        first, size = own_first(count), count * rows
+        total = pair_sum[at_row((first - side * chips) * rows, size), :].astype(F32)
+        for d in range(1, chips):
+            z = lax.rem(chip + d, chips)
+            pltpu.make_async_remote_copy(
+                src_ref=rs_in.at[z, pl.ds(0, size)],
+                dst_ref=rs_in.at[z, pl.ds(0, size)],
+                send_sem=rs_s.at[z],
+                recv_sem=rs_r.at[z],
+                device_id={"pw": 2 * z + side},
+                device_id_type=MESH,
+            ).wait_recv()
+            total = total + rs_in[z, 0:size, :].astype(F32)
+        p_all[at_row(first * rows, size), :] = total.astype(BF)
+        pairs = []
+        for k in range(0, size, 8):
+            left = total[k : k + 8, :] * weights
+            pair = jnp.concatenate(
+                [jnp.broadcast_to(total[k + i : k + i + 1, :], (8, 2 * bands)) * left for i in range(8)],
+                axis=0,
+            ).astype(BF)
+            pairs += [pair, pair]
+        flat = lax.dot_general(
+            jnp.ones((16, 2 * bands), BF),
+            jnp.concatenate(pairs, axis=0),
+            (((1,), (1,)), ((), ())),
+            preferred_element_type=F32,
+        )
+        for k in range(count * own):
+            o_in[mb * n + first + k // own, k % own : k % own + 1, :] = flat[0:1, k * 128 : k * 128 + 128]
+        wait_go()
+        each_peer(lambda to, band, at: occupancy_copy(to, band, at, first, count).start())
+        for i in range(n - 1):
+            projection_copy(i, first, count).start()
+
+    each_role(share)
+    for c in range(0, half, chunk):
+        swap(c).wait_send()
+    for z in range(single + double):
+        @pl.when(z != chip)
+        def _():
+            scatter(z).wait_send()
+
+    def drain(count):
+        if count:
+            first = own_first(count)
+            each_peer(lambda to, band, at: occupancy_copy(to, band, at, first, count).wait_send())
+            for i in range(n - 1):
+                projection_copy(i, first, count).wait_send()
+
+    each_role(drain)
+    def wait_occupancies(count):
+        pltpu.make_async_copy(
+            o_in.at[pl.ds(0, nb * n - count)], o_in.at[pl.ds(0, nb * n - count)], oc_r
+        ).wait()
+
+    each_role(wait_occupancies)
     for d in range(n):
-        summed = o_in[0, d]
+        summed = o_in[d]
         for b in range(1, nb):
-            summed = summed + o_in[b, d]
+            summed = summed + o_in[b * n + d]
         o_sum[d * own : d * own + own, :] = summed
     matrix = []
     for q in range(0, atoms, group):
@@ -333,16 +471,11 @@
         answer = jnp.where(diagonal, answer + bare[q * 8 : q * 8 + span, :], 0.0)
         folded[q * 8 : q * 8 + span, :] = answer
         matrix.append(answer.astype(BF))
-    for s in range(1, n):
-        owner = lax.rem(me + s, n)
-        pltpu.make_async_remote_copy(
-            src_ref=p_all.at[block(owner)],
-            dst_ref=p_all.at[block(owner)],
-            send_sem=ag_s.at[0],
-            recv_sem=ag_r.at[owner],
-            device_id={"pw": owner},
-            device_id_type=MESH,
-        ).wait_recv()
+    def wait_projections(count):
+        got = p_all.at[pl.ds(0, every - count * rows)]
+        pltpu.make_async_copy(got, got, ag_r).wait()
+
+    each_role(wait_projections)
     for q in range(0, every, span):
         w = jnp.dot(matrix[q // span], p_all[q : q + span, :], preferred_element_type=F32)
         w = w.astype(BF)
@@ -352,12 +485,9 @@
     result = jnp.dot(beta_t[...], ww[...], preferred_element_type=F32).astype(BF)
     applied[0] = result[:, 0:bands]
     applied[1] = result[:, bands : 2 * bands]
-    mine = jnp.dot(folded[block(me), :], fold, precision=HIGH, preferred_element_type=F32)
+    mine = jnp.dot(folded[at_row((side * chips + chip) * rows, rows), :], fold, precision=HIGH, preferred_element_type=F32)
     for k in range(own):
         onsite[k] = mine[k * 8 : k * 8 + 8, :]
-    for copy in sends + p_sends:
-        copy.wait_send()
-    each_peer(lambda to, band, at: occupancy_copy(to, band, me, mb, at).wait_send())
 
 
 def finish(applied_in, onsite_in, applied, onsite, sem):
@@ -380,6 +510,7 @@
         own = atoms // n
         rows, every = own * 8, atoms * 8
         span = min(atoms, 32) * 8
+        half = every // 2
         kinds = widths.shape[0]
         vmem = pl.BlockSpec(memory_space=pltpu.VMEM)
         hbm = pl.BlockSpec(memory_space=pltpu.HBM)
@@ -410,10 +541,13 @@
                 pltpu.VMEM((kinds, 8, npw), F32),
                 pltpu.VMEM((every, 2 * npw), BF),
                 pltpu.VMEM((npw, 2 * every), BF),
+                pltpu.VMEM((half, 2 * bands), BF),
+                pltpu.VMEM((half, 2 * bands), F32),
+                pltpu.VMEM((half, 2 * bands), BF),
+                pltpu.VMEM((half, 2 * bands), BF),
+                pltpu.VMEM((n // 2, 2 * rows, 2 * bands), BF),
                 pltpu.VMEM((every, 2 * bands), BF),
-                pltpu.VMEM((n, rows, 2 * bands), BF),
-                pltpu.VMEM((every, 2 * bands), BF),
-                pltpu.VMEM((nb, n, own, 128), F32),
+                pltpu.VMEM((nb * n, own, 128), F32),
                 pltpu.VMEM((atoms, 128), F32),
                 pltpu.VMEM((kinds, 8, span), F32),
                 pltpu.VMEM((kinds, 8, 512), F32),
@@ -423,12 +557,17 @@
                 pltpu.VMEM((every, span), F32),
                 pltpu.VMEM((2 * every, 2 * bands), BF),
                 dma((12,)),
+                dma((half // (2 * rows),)),
+                dma((half // (2 * rows),)),
+                dma((n // 2,)),
+                dma((n // 2,)),
                 dma((n,)),
-                dma((n,)),
-                dma((n,)),
-                dma((n,)),
+                dma,
                 dma((n * nb,)),
-                dma((n * nb,)),
+                dma,
+                pltpu.SemaphoreType.REGULAR,
+                pltpu.SemaphoreType.REGULAR((n,)),
+                pltpu.SemaphoreType.REGULAR,
                 pltpu.SemaphoreType.REGULAR,
             ],
             compiler_params=pltpu.CompilerParams(

time: 18.6 us -> 17.5 us (0.941)
  Pallas kernels: 17.7 us -> 16.6 us
    pallas_call x1, Pallas kernels: 17 us -> 15.9 us  [local(): pl.pallas_call(functools.partial(kernel, n, nb), out_shape=results, in_sp...]
where the time goes in v2:
time: 17.5 us; the launch traced here: 17.3 us
  Pallas kernels  16.6 us (95%)
  between operations  0.64 us (4%)
    pallas_call x1, Pallas kernels, local(): pl.pallas_call(functools.partial(kernel, n, nb), out_shape=results, in_sp...  15.9 us
    pallas_call x1, Pallas kernels, local(): pl.pallas_call(finish, out_shape=results, in_specs=[anywhere] * 2, out_sp...  0.72 us

profile of v2, /device:TPU:0, one launch (start us, length us, event | category | flops | bytes accessed | tf_op | source)
XLA Modules:
  0.0 17.3 jit_solution(5431751720398957546)
XLA Ops:
  0.6 15.9 %shard_map.113 = (bf16[2,512,128]{2,1,0:T(8,128)(2,1)S(1)}, f32[4,8,8]{2,1,0:T(8,128)S(1)}) custom-call(bf16[2,512,128]{2,1,0:T(8,128)(2,1)} %wave.1, s32[3,512]{1,0:T(4,128)} %miller_h.1, f32[3,3]{1,0:T(4,128)} %reciprocal_h.1, f32[3,32]{1,0:T(4,128)} %fractional_h.1, s32[32]{0:T(128)} %species_h.1, s32[32]{0:T(128)} %order_h.1, f32[4,4]{1,0:T(4,128)} %widths_h.1, ...), custom_call_target="tpu_custom_call" | custom-call | tf_op jit(solution)/shard_map/pallas_call | solution.py:522
  16.5 0.7 %shard_map.114 = (bf16[2,512,128]{2,1,0:T(8,128)(2,1)}, f32[4,8,8]{2,1,0:T(8,128)}) custom-call(bf16[2,512,128]{2,1,0:T(8,128)(2,1)S(1)} %get-tuple-element.4.applied_in, f32[4,8,8]{2,1,0:T(8,128)S(1)} %get-tuple-element.5.onsite_in), custom_call_target="tpu_custom_call" | custom-call | tf_op jit(solution)/shard_map/pallas_call | solution.py:594
